TPU v7x, 32 devices: a whole 2x2x4 slice. The times are simulated.
32 devices in a mesh: row: 4 (over z), col: 8 (over y, x, core).
Axes of the slice: x: 2, y: 2, z: 4, core: 2. Of those that a mesh axis runs over, the one named last changes fastest.
Arguments:
- losses: float32 [8, 16384], P(None, ('row', 'col')), may hold values from 0.05 to 12
- domains: int32 [8, 16384], P(None, ('row', 'col')), may hold values from 0 to 2047
Outputs:
- token_count: float32 [8, 2048], replicated
- loss_mean: float32 [8, 2048], replicated
- loss_variance: float32 [8, 2048], replicated
All inputs are finite; a program needn't handle non-finite values.
Results may differ from a plain program's by a relative error of at most 0.0001.
Values sent between devices are 32-bit elements; how exact they have to be, the bound alone decides.
A program may use at most 64 MiB of HBM per device.

v0:
```python
import jax
import jax.numpy as jnp
from jax import lax
from jax.sharding import PartitionSpec as P

DOMAINS = 2048


HIGHEST = lax.Precision.HIGHEST


def merged_2(value, axis, join):
    pieces = jax.tree.map(lambda part: lax.all_gather(part, axis), value)
    head = jax.tree.map(lambda part: part[0], pieces)
    tail = jax.tree.map(lambda part: part[1:], pieces)
    total, _ = lax.scan(lambda total, piece: (join(total, piece), None), head, tail)
    return total


def combine_moments(first, second):
    count_a, mean_a, spread_a = first
    count_b, mean_b, spread_b = second
    count = count_a + count_b
    inverse = 1.0 / jnp.maximum(count, 1.0)
    delta = mean_b - mean_a
    mean = mean_a + delta * (count_b * inverse)
    spread = spread_a + spread_b + delta * delta * (count_a * count_b * inverse)
    return (count, mean, spread)


def block_rows():
    return 512


def one_hot(id_block, width):
    columns = lax.broadcasted_iota(jnp.int32, (1, width), 1)
    return (id_block[:, None] == columns).astype(jnp.float32)


def count_and_total(loss_row, id_row):
    size = block_rows()
    loss_blocks = loss_row.reshape(-1, size)
    id_blocks = id_row.reshape(-1, size)

    def count_add_block(index, accum):
        values = loss_blocks[index]
        hot = one_hot(id_blocks[index], DOMAINS)
        stacked = jnp.stack([jnp.ones_like(values), values])
        return accum + jnp.dot(stacked, hot, precision=HIGHEST, preferred_element_type=jnp.float32)

    start = jnp.zeros((2, DOMAINS), jnp.float32)
    return lax.fori_loop(0, loss_blocks.shape[0], count_add_block, start)


def centred_squares(loss_row, id_row, centre):
    size = block_rows()
    loss_blocks = loss_row.reshape(-1, size)
    id_blocks = id_row.reshape(-1, size)

    def centred_add_block(index, accum):
        hot = one_hot(id_blocks[index], DOMAINS)
        looked = jnp.dot(hot, centre, precision=HIGHEST, preferred_element_type=jnp.float32)
        deviation = loss_blocks[index] - looked
        return accum + jnp.dot(
            deviation * deviation, hot, precision=HIGHEST, preferred_element_type=jnp.float32
        )

    start = jnp.zeros((DOMAINS,), jnp.float32)
    return lax.fori_loop(0, loss_blocks.shape[0], centred_add_block, start)


def local_moments(losses, domains):

    def per_micro(carry, inputs):
        loss_row, id_row = inputs
        sums = count_and_total(loss_row, id_row)
        count = sums[0]
        mean = sums[1] / jnp.maximum(count, 1.0)
        spread = centred_squares(loss_row, id_row, mean)
        return (carry, (count, mean, spread))

    return lax.scan(per_micro, 0.0, (losses, domains))[1]


def finish(count, mean, spread):
    variance = spread / jnp.maximum(count - 1.0, 1.0)
    return (count, mean, variance)


def on_device(losses, domains):
    count, mean, spread = local_moments(losses, domains)
    partial_count, partial_mean, partial_spread = merged_2(
        (count, mean, spread), "col", combine_moments
    )
    merged = merged_2((partial_count, partial_mean, partial_spread), "row", combine_moments)
    return finish(merged[0], merged[1], merged[2])


def solution(mesh):
    return jax.shard_map(
        on_device,
        mesh=mesh,
        in_specs=(P(None, ("row", "col")), P(None, ("row", "col"))),
        out_specs=(P(), P(), P()),
        check_vma=False,
    )
```

profile of v0, /device:TPU:0, one launch (start us, length us, event | category | flops | bytes accessed | tf_op | source)
XLA Modules:
  0.0 135.3 jit_solution(4821769083579554170)
XLA Ops:
  0.7 56.5 %while.8 = (s32[]{:T(128)}, f32[8,2048]{1,0:T(8,128)S(1)}, f32[8,2048]{1,0:T(8,128)S(1)}, f32[8,2048]{1,0:T(8,128)S(1)}, f32[8,512]{1,0:T(8,128)}, /*index=5*/s32[8,512]{1,0:T(8,128)}, s32[]{:T(128)}, s32[]{:T(128)}) while((s32[]{:T(128)}, f32[8,2048]{1,0:T(8,128)S(1)}, f32[8,2048]{1,0:T(8,128)S(1)}, f32[8,2048]{1,0:T(8,128)S(1)}, ...), condition=%wide.region_1.2_spmd, body=%wide.region_0.1_spmd.sunk | while | flops 53482496 | bytes 141425 | solution.py:82
  0.7 0.7 constant_dynamic-slice_fusion.5
  1.4 0.7 constant_dynamic-slice_fusion.4
  2.1 1.5 %fusion.33 = f32[2,2048]{1,0:T(2,128)S(1)} fusion(s32[512]{0:T(512)S(1)} %bitcast.107, f32[1,512]{1,0:T(1,128)S(1)} %constant_dynamic-slice_fusion.5), kind=kOutput, calls=%fused_computation.3.clone.1 | convolution fusion | flops 26214400 | bytes 20480 | tf_op jit(solution)/shard_map/while/body/eval_jaxpr/while/body/eval_jaxpr/dot_general | solution.py:49
  3.6 2.0 %fusion.34 = f32[1,512]{1,0:T(1,128)S(1)} fusion(s32[512]{0:T(512)S(1)} %bitcast.108, f32[1,2048]{1,0:T(1,128)S(1)} %get-tuple-element.319), kind=kOutput, calls=%fused_computation.2.clone.1 | convolution fusion | flops 13631488 | bytes 12288 | tf_op jit(solution)/shard_map/while/body/eval_jaxpr/while/body/eval_jaxpr/dot_general | solution.py:62
  5.6 1.5 %fusion.35 = f32[1,2048]{1,0:T(1,128)S(1)} fusion(f32[512,1]{0,1:T(1,128)S(1)} %bitcast.105, s32[512]{0:T(512)S(1)} %bitcast.109), kind=kOutput, calls=%fused_computation.1.clone.1 | convolution fusion | flops 13631488 | bytes 12288 | tf_op jit(solution)/shard_map/while/body/eval_jaxpr/while/body/eval_jaxpr/dot_general | solution.py:64
  7.7 0.7 constant_dynamic-slice_fusion.5
  8.5 0.7 constant_dynamic-slice_fusion.4
  9.2 1.5 %fusion.33 = f32[2,2048]{1,0:T(2,128)S(1)} fusion(s32[512]{0:T(512)S(1)} %bitcast.107, f32[1,512]{1,0:T(1,128)S(1)} %constant_dynamic-slice_fusion.5), kind=kOutput, calls=%fused_computation.3.clone.1 | convolution fusion | flops 26214400 | bytes 20480 | tf_op jit(solution)/shard_map/while/body/eval_jaxpr/while/body/eval_jaxpr/dot_general | solution.py:49
  10.7 2.0 %fusion.34 = f32[1,512]{1,0:T(1,128)S(1)} fusion(s32[512]{0:T(512)S(1)} %bitcast.108, f32[1,2048]{1,0:T(1,128)S(1)} %get-tuple-element.319), kind=kOutput, calls=%fused_computation.2.clone.1 | convolution fusion | flops 13631488 | bytes 12288 | tf_op jit(solution)/shard_map/while/body/eval_jaxpr/while/body/eval_jaxpr/dot_general | solution.py:62
  12.7 1.5 %fusion.35 = f32[1,2048]{1,0:T(1,128)S(1)} fusion(f32[512,1]{0,1:T(1,128)S(1)} %bitcast.105, s32[512]{0:T(512)S(1)} %bitcast.109), kind=kOutput, calls=%fused_computation.1.clone.1 | convolution fusion | flops 13631488 | bytes 12288 | tf_op jit(solution)/shard_map/while/body/eval_jaxpr/while/body/eval_jaxpr/dot_general | solution.py:64
  14.8 0.7 constant_dynamic-slice_fusion.5
  15.5 0.7 constant_dynamic-slice_fusion.4
  16.3 1.5 %fusion.33 = f32[2,2048]{1,0:T(2,128)S(1)} fusion(s32[512]{0:T(512)S(1)} %bitcast.107, f32[1,512]{1,0:T(1,128)S(1)} %constant_dynamic-slice_fusion.5), kind=kOutput, calls=%fused_computation.3.clone.1 | convolution fusion | flops 26214400 | bytes 20480 | tf_op jit(solution)/shard_map/while/body/eval_jaxpr/while/body/eval_jaxpr/dot_general | solution.py:49
  17.8 2.0 %fusion.34 = f32[1,512]{1,0:T(1,128)S(1)} fusion(s32[512]{0:T(512)S(1)} %bitcast.108, f32[1,2048]{1,0:T(1,128)S(1)} %get-tuple-element.319), kind=kOutput, calls=%fused_computation.2.clone.1 | convolution fusion | flops 13631488 | bytes 12288 | tf_op jit(solution)/shard_map/while/body/eval_jaxpr/while/body/eval_jaxpr/dot_general | solution.py:62
  19.8 1.5 %fusion.35 = f32[1,2048]{1,0:T(1,128)S(1)} fusion(f32[512,1]{0,1:T(1,128)S(1)} %bitcast.105, s32[512]{0:T(512)S(1)} %bitcast.109), kind=kOutput, calls=%fused_computation.1.clone.1 | convolution fusion | flops 13631488 | bytes 12288 | tf_op jit(solution)/shard_map/while/body/eval_jaxpr/while/body/eval_jaxpr/dot_general | solution.py:64
  21.9 0.7 constant_dynamic-slice_fusion.5
  23.3 1.5 %fusion.33 = f32[2,2048]{1,0:T(2,128)S(1)} fusion(s32[512]{0:T(512)S(1)} %bitcast.107, f32[1,512]{1,0:T(1,128)S(1)} %constant_dynamic-slice_fusion.5), kind=kOutput, calls=%fused_computation.3.clone.1 | convolution fusion | flops 26214400 | bytes 20480 | tf_op jit(solution)/shard_map/while/body/eval_jaxpr/while/body/eval_jaxpr/dot_general | solution.py:49
  24.8 2.0 %fusion.34 = f32[1,512]{1,0:T(1,128)S(1)} fusion(s32[512]{0:T(512)S(1)} %bitcast.108, f32[1,2048]{1,0:T(1,128)S(1)} %get-tuple-element.319), kind=kOutput, calls=%fused_computation.2.clone.1 | convolution fusion | flops 13631488 | bytes 12288 | tf_op jit(solution)/shard_map/while/body/eval_jaxpr/while/body/eval_jaxpr/dot_general | solution.py:62
  26.8 1.5 %fusion.35 = f32[1,2048]{1,0:T(1,128)S(1)} fusion(f32[512,1]{0,1:T(1,128)S(1)} %bitcast.105, s32[512]{0:T(512)S(1)} %bitcast.109), kind=kOutput, calls=%fused_computation.1.clone.1 | convolution fusion | flops 13631488 | bytes 12288 | tf_op jit(solution)/shard_map/while/body/eval_jaxpr/while/body/eval_jaxpr/dot_general | solution.py:64
  28.9 0.7 constant_dynamic-slice_fusion.5
  30.4 1.5 %fusion.33 = f32[2,2048]{1,0:T(2,128)S(1)} fusion(s32[512]{0:T(512)S(1)} %bitcast.107, f32[1,512]{1,0:T(1,128)S(1)} %constant_dynamic-slice_fusion.5), kind=kOutput, calls=%fused_computation.3.clone.1 | convolution fusion | flops 26214400 | bytes 20480 | tf_op jit(solution)/shard_map/while/body/eval_jaxpr/while/body/eval_jaxpr/dot_general | solution.py:49
  31.9 2.0 %fusion.34 = f32[1,512]{1,0:T(1,128)S(1)} fusion(s32[512]{0:T(512)S(1)} %bitcast.108, f32[1,2048]{1,0:T(1,128)S(1)} %get-tuple-element.319), kind=kOutput, calls=%fused_computation.2.clone.1 | convolution fusion | flops 13631488 | bytes 12288 | tf_op jit(solution)/shard_map/while/body/eval_jaxpr/while/body/eval_jaxpr/dot_general | solution.py:62
  33.9 1.5 %fusion.35 = f32[1,2048]{1,0:T(1,128)S(1)} fusion(f32[512,1]{0,1:T(1,128)S(1)} %bitcast.105, s32[512]{0:T(512)S(1)} %bitcast.109), kind=kOutput, calls=%fused_computation.1.clone.1 | convolution fusion | flops 13631488 | bytes 12288 | tf_op jit(solution)/shard_map/while/body/eval_jaxpr/while/body/eval_jaxpr/dot_general | solution.py:64
  36.0 0.7 constant_dynamic-slice_fusion.5
  37.5 1.5 %fusion.33 = f32[2,2048]{1,0:T(2,128)S(1)} fusion(s32[512]{0:T(512)S(1)} %bitcast.107, f32[1,512]{1,0:T(1,128)S(1)} %constant_dynamic-slice_fusion.5), kind=kOutput, calls=%fused_computation.3.clone.1 | convolution fusion | flops 26214400 | bytes 20480 | tf_op jit(solution)/shard_map/while/body/eval_jaxpr/while/body/eval_jaxpr/dot_general | solution.py:49
  39.0 2.0 %fusion.34 = f32[1,512]{1,0:T(1,128)S(1)} fusion(s32[512]{0:T(512)S(1)} %bitcast.108, f32[1,2048]{1,0:T(1,128)S(1)} %get-tuple-element.319), kind=kOutput, calls=%fused_computation.2.clone.1 | convolution fusion | flops 13631488 | bytes 12288 | tf_op jit(solution)/shard_map/while/body/eval_jaxpr/while/body/eval_jaxpr/dot_general | solution.py:62
  41.0 1.5 %fusion.35 = f32[1,2048]{1,0:T(1,128)S(1)} fusion(f32[512,1]{0,1:T(1,128)S(1)} %bitcast.105, s32[512]{0:T(512)S(1)} %bitcast.109), kind=kOutput, calls=%fused_computation.1.clone.1 | convolution fusion | flops 13631488 | bytes 12288 | tf_op jit(solution)/shard_map/while/body/eval_jaxpr/while/body/eval_jaxpr/dot_general | solution.py:64
  43.1 0.7 constant_dynamic-slice_fusion.5
  43.8 0.7 constant_dynamic-slice_fusion.4
  44.5 1.5 %fusion.33 = f32[2,2048]{1,0:T(2,128)S(1)} fusion(s32[512]{0:T(512)S(1)} %bitcast.107, f32[1,512]{1,0:T(1,128)S(1)} %constant_dynamic-slice_fusion.5), kind=kOutput, calls=%fused_computation.3.clone.1 | convolution fusion | flops 26214400 | bytes 20480 | tf_op jit(solution)/shard_map/while/body/eval_jaxpr/while/body/eval_jaxpr/dot_general | solution.py:49
  46.0 2.0 %fusion.34 = f32[1,512]{1,0:T(1,128)S(1)} fusion(s32[512]{0:T(512)S(1)} %bitcast.108, f32[1,2048]{1,0:T(1,128)S(1)} %get-tuple-element.319), kind=kOutput, calls=%fused_computation.2.clone.1 | convolution fusion | flops 13631488 | bytes 12288 | tf_op jit(solution)/shard_map/while/body/eval_jaxpr/while/body/eval_jaxpr/dot_general | solution.py:62
  48.0 1.5 %fusion.35 = f32[1,2048]{1,0:T(1,128)S(1)} fusion(f32[512,1]{0,1:T(1,128)S(1)} %bitcast.105, s32[512]{0:T(512)S(1)} %bitcast.109), kind=kOutput, calls=%fused_computation.1.clone.1 | convolution fusion | flops 13631488 | bytes 12288 | tf_op jit(solution)/shard_map/while/body/eval_jaxpr/while/body/eval_jaxpr/dot_general | solution.py:64
  50.1 0.7 constant_dynamic-slice_fusion.5
  51.6 1.5 %fusion.33 = f32[2,2048]{1,0:T(2,128)S(1)} fusion(s32[512]{0:T(512)S(1)} %bitcast.107, f32[1,512]{1,0:T(1,128)S(1)} %constant_dynamic-slice_fusion.5), kind=kOutput, calls=%fused_computation.3.clone.1 | convolution fusion | flops 26214400 | bytes 20480 | tf_op jit(solution)/shard_map/while/body/eval_jaxpr/while/body/eval_jaxpr/dot_general | solution.py:49
  53.1 2.0 %fusion.34 = f32[1,512]{1,0:T(1,128)S(1)} fusion(s32[512]{0:T(512)S(1)} %bitcast.108, f32[1,2048]{1,0:T(1,128)S(1)} %get-tuple-element.319), kind=kOutput, calls=%fused_computation.2.clone.1 | convolution fusion | flops 13631488 | bytes 12288 | tf_op jit(solution)/shard_map/while/body/eval_jaxpr/while/body/eval_jaxpr/dot_general | solution.py:62
  55.1 1.5 %fusion.35 = f32[1,2048]{1,0:T(1,128)S(1)} fusion(f32[512,1]{0,1:T(1,128)S(1)} %bitcast.105, s32[512]{0:T(512)S(1)} %bitcast.109), kind=kOutput, calls=%fused_computation.1.clone.1 | convolution fusion | flops 13631488 | bytes 12288 | tf_op jit(solution)/shard_map/while/body/eval_jaxpr/while/body/eval_jaxpr/dot_general | solution.py:64
  57.2 11.3 %all-gather.2 = f32[64,2048]{1,0:T(8,128)S(1)} all-gather(f32[8,2048]{1,0:T(8,128)S(1)} %get-tuple-element.150), channel_id=4, replica_groups=mesh['row'=4,'col'=8] {'col'}, dimensions={0}, use_global_device_ids=true | all-gather | bytes 589824 | tf_op jit(solution)/shard_map/all_gather | solution.py:13
  68.6 0.8 copy-done.3
  69.3 9.8 %all-gather = f32[64,2048]{1,0:T(8,128)S(1)} all-gather(f32[8,2048]{1,0:T(8,128)S(1)} %get-tuple-element.148), channel_id=2, replica_groups=mesh['row'=4,'col'=8] {'col'}, dimensions={0}, use_global_device_ids=true | all-gather | bytes 589824 | tf_op jit(solution)/shard_map/all_gather | solution.py:13
  79.2 0.8 copy-done
  80.0 8.9 %all-gather.1 = f32[64,2048]{1,0:T(8,128)S(1)} all-gather(f32[8,2048]{1,0:T(8,128)S(1)} %get-tuple-element.149), channel_id=3, replica_groups=mesh['row'=4,'col'=8] {'col'}, dimensions={0}, use_global_device_ids=true | all-gather | bytes 589824 | tf_op jit(solution)/shard_map/all_gather | solution.py:13
  88.9 0.8 slice-done
  89.7 0.8 while.9
  90.5 14.1 %all-gather.5 = f32[32,2048]{1,0:T(8,128)S(1)} all-gather(f32[8,2048]{1,0:T(8,128)S(1)} %get-tuple-element.153), channel_id=7, replica_groups=mesh['row'=4,'col'=8] {'row'}, dimensions={0}, use_global_device_ids=true | all-gather | bytes 327680 | tf_op jit(solution)/shard_map/all_gather | solution.py:13
  104.6 14.6 %all-gather.3 = f32[32,2048]{1,0:T(8,128)S(1)} all-gather(f32[8,2048]{1,0:T(8,128)S(1)} %get-tuple-element.151), channel_id=5, replica_groups=mesh['row'=4,'col'=8] {'row'}, dimensions={0}, use_global_device_ids=true | all-gather | bytes 327680 | tf_op jit(solution)/shard_map/all_gather | solution.py:13
  119.3 14.1 %all-gather.4 = f32[32,2048]{1,0:T(8,128)S(1)} all-gather(f32[8,2048]{1,0:T(8,128)S(1)} %get-tuple-element.152), channel_id=6, replica_groups=mesh['row'=4,'col'=8] {'row'}, dimensions={0}, use_global_device_ids=true | all-gather | bytes 327680 | tf_op jit(solution)/shard_map/all_gather | solution.py:13
  133.4 0.8 slice-done.2
  (90 shorter events, 10.0 us)
Async XLA Ops:
  68.5 0.8 copy-start.3
  79.2 0.8 copy-start
  88.8 0.8 slice-start
  88.8 0.9 slice-start.1
  104.6 14.7 %copy-start.4 = (f32[32,2048]{1,0:T(8,128)}, f32[32,2048]{1,0:T(8,128)S(1)}, u32[]{:S(2)}) copy-start(f32[32,2048]{1,0:T(8,128)S(1)} %all-gather.5) | copy-start | bytes 786436
  133.4 0.8 slice-start.2
  134.6 0.7 copy-start.1
  134.6 0.7 copy-start.2
where the time goes:
time: 137 us; the launch traced here: 135 us
  blocking collectives  72.8 us (53%)
  matrix products  39.6 us (29%)
  local copies, waits for them, and re-layouts  19.6 us (14%)
  other arithmetic  1.87 us (1%)
    all_gather x6, blocking collectives, merged_2(): pieces = jax.tree.map(lambda part: lax.all_gather(part, axis), value)  72.8 us
    dot_general x8, matrix products, centred_add_block(): jnp.dot(hot, centre, precision=HIGHEST, preferred_element_type=jnp.float32)  16.1 us
    dot_general x8, matrix products, centred_add_block(): jnp.dot(deviation * deviation, hot, precision=HIGHEST, preferred_element_...  11.8 us
    dot_general x8, matrix products, count_add_block(): jnp.dot(stacked, hot, precision=HIGHEST, preferred_element_type=jnp.float32)  11.7 us
    dynamic_slice x16, local copies, waits for them, and re-layouts, local_moments(): return lax.scan(per_micro, 0.0, (losses, domains))[1]  11.6 us
    dynamic_update_slice x24, local copies, waits for them, and re-layouts, local_moments(): return lax.scan(per_micro, 0.0, (losses, domains))[1]  4.69 us

commit v1 on v0

v1 whole, which is shorter than its diff:
```python
import functools

import jax
import jax.numpy as jnp
from jax import lax
from jax.experimental import pallas as pl
from jax.experimental.pallas import tpu as pltpu
from jax.sharding import PartitionSpec as P

DOMAINS = 2048
LANES = 128
MESH = pl.DeviceIdType.MESH


def pieces(value):
    first = value.astype(jnp.bfloat16).astype(jnp.float32)
    rest = value - first
    second = rest.astype(jnp.bfloat16).astype(jnp.float32)
    return first, second, rest - second


def nt_dot(a, b):
    return lax.dot_general(a, b, (((1,), (1,)), ((), ())), preferred_element_type=jnp.float32)


def local_stats(loss, ids, groups):
    tokens = loss.shape[1]
    low = lax.bitwise_and(ids, LANES - 1)
    high = lax.shift_right_logical(ids, LANES.bit_length() - 1)
    low_hot = (lax.broadcasted_iota(jnp.int32, (LANES, tokens), 0) == low).astype(jnp.float32).astype(jnp.bfloat16)
    in_group = lax.broadcasted_iota(jnp.int32, (groups, tokens), 0) == high

    def spread_out(row):
        return jnp.where(in_group, row, 0.0).astype(jnp.bfloat16)

    first = jnp.concatenate([spread_out(row) for row in (jnp.ones_like(loss),) + pieces(loss)], axis=0)
    sums = nt_dot(first, low_hot)
    count = sums[:groups]
    total = sums[groups:2 * groups] + sums[2 * groups:3 * groups] + sums[3 * groups:]
    mean = total / jnp.maximum(count, 1.0)
    parts = jnp.concatenate([part.astype(jnp.bfloat16) for part in pieces(mean)], axis=0)
    looked = jnp.dot(parts, low_hot, preferred_element_type=jnp.float32)
    looked = looked[:groups] + looked[groups:2 * groups] + looked[2 * groups:]
    centre = jnp.sum(jnp.where(in_group, looked, 0.0), axis=0, keepdims=True)
    deviation = loss - centre
    squares = jnp.concatenate([spread_out(row) for row in pieces(deviation * deviation)], axis=0)
    sums = nt_dot(squares, low_hot)
    spread = sums[:groups] + sums[groups:2 * groups] + sums[2 * groups:]
    return count, total, spread


def kernel(
    axes, sizes, owners, rows, loss_ref, ids_ref, count_ref, mean_ref, variance_ref,
    send, recv, final, send_sem, recv_sem, out_sem, final_sem,
):
    n = sizes[0] * sizes[1]
    micro = loss_ref.shape[0]
    groups = DOMAINS // LANES
    me = lax.axis_index(axes[0]) * sizes[1] + lax.axis_index(axes[1])

    def coordinates(device):
        return (device // sizes[1], device % sizes[1])

    def other(step):
        return lax.rem(me + step, n)

    barrier = pltpu.get_barrier_semaphore()

    @pl.loop(1, n)
    def _(step):
        pl.semaphore_signal(barrier, inc=1, device_id=coordinates(other(step)), device_id_type=MESH)

    for m in range(micro):
        stats = local_stats(loss_ref[m:m + 1, :], ids_ref[m:m + 1, :], groups)
        for part in range(groups // rows):
            owner = m * (groups // rows) + part
            for which, stat in enumerate(stats):
                send[owner, which * rows:(which + 1) * rows, :] = stat[part * rows:(part + 1) * rows]

    pl.semaphore_wait(barrier, n - 1)

    def to_owner(device):
        return pltpu.make_async_remote_copy(
            src_ref=send.at[device], dst_ref=recv.at[me],
            send_sem=send_sem.at[device], recv_sem=recv_sem.at[me],
            device_id=coordinates(device), device_id_type=MESH,
        )

    def from_device(device):
        return pltpu.make_async_remote_copy(
            src_ref=recv.at[device], dst_ref=recv.at[device],
            send_sem=recv_sem.at[device], recv_sem=recv_sem.at[device],
            device_id=coordinates(device), device_id_type=MESH,
        )

    def to_everyone(device):
        return pltpu.make_async_remote_copy(
            src_ref=final.at[me], dst_ref=final.at[me],
            send_sem=out_sem.at[device], recv_sem=final_sem.at[me],
            device_id=coordinates(device), device_id_type=MESH,
        )

    def from_owner(device):
        return pltpu.make_async_remote_copy(
            src_ref=final.at[device], dst_ref=final.at[device],
            send_sem=final_sem.at[device], recv_sem=final_sem.at[device],
            device_id=coordinates(device), device_id_type=MESH,
        )

    def if_owner(device, action):
        if owners == n:
            action()
        else:
            pl.when(device < owners)(action)

    @pl.loop(1, n)
    def _(step):
        device = other(step)
        if_owner(device, lambda: to_owner(device).start())

    def combine():
        recv[me] = send[me]

        @pl.loop(1, n)
        def _(step):
            from_device(other(step)).wait_recv()

        counts = recv[:, :rows, :]
        totals = recv[:, rows:2 * rows, :]
        count = jnp.sum(counts, axis=0)
        mean = jnp.sum(totals, axis=0) / jnp.maximum(count, 1.0)
        gap = totals / jnp.maximum(counts, 1.0) - mean[None]
        spread = jnp.sum(recv[:, 2 * rows:, :] + counts * (gap * gap), axis=0)
        final[me, :rows, :] = count
        final[me, rows:2 * rows, :] = mean
        final[me, 2 * rows:, :] = spread / jnp.maximum(count - 1.0, 1.0)

        @pl.loop(1, n)
        def _(step):
            to_everyone(other(step)).start()

    if_owner(me, combine)

    @pl.loop(1, n)
    def _(step):
        device = other(step)
        if_owner(device, lambda: from_owner(device).wait_recv())

    stride = groups // rows
    for which, out in enumerate((count_ref, mean_ref, variance_ref)):
        for group in range(groups):
            row = which * rows + group % rows
            block = [final[m * stride + group // rows, row:row + 1, :] for m in range(micro)]
            out[:, group * LANES:(group + 1) * LANES] = jnp.concatenate(block, axis=0)

    @pl.loop(1, n)
    def _(step):
        device = other(step)
        if_owner(device, lambda: to_owner(device).wait_send())
        if_owner(me, lambda: to_everyone(device).wait_send())


def solution(mesh):
    axes = tuple(mesh.axis_names)
    sizes = tuple(mesh.shape[axis] for axis in axes)
    n = sizes[0] * sizes[1]

    def on_device(losses, domains):
        micro = losses.shape[0]
        all_rows = micro * (DOMAINS // LANES)
        rows = max(1, all_rows // n)
        owners = all_rows // rows
        out = jax.ShapeDtypeStruct((micro, DOMAINS), jnp.float32)
        return pl.pallas_call(
            functools.partial(kernel, axes, sizes, owners, rows),
            out_shape=(out, out, out),
            in_specs=[pl.BlockSpec(memory_space=pltpu.VMEM)] * 2,
            out_specs=[pl.BlockSpec(memory_space=pltpu.VMEM)] * 3,
            scratch_shapes=[
                pltpu.VMEM((owners, 3 * rows, LANES), jnp.float32),
                pltpu.VMEM((n, 3 * rows, LANES), jnp.float32),
                pltpu.VMEM((owners, 3 * rows, LANES), jnp.float32),
                pltpu.SemaphoreType.DMA((owners,)),
                pltpu.SemaphoreType.DMA((n,)),
                pltpu.SemaphoreType.DMA((n,)),
                pltpu.SemaphoreType.DMA((owners,)),
            ],
            compiler_params=pltpu.CompilerParams(collective_id=0, has_side_effects=True),
        )(losses, domains)

    return jax.shard_map(
        on_device,
        mesh=mesh,
        in_specs=(P(None, axes), P(None, axes)),
        out_specs=(P(), P(), P()),
        check_vma=False,
    )
```

time: 137 us -> 25.8 us (0.19); the launches traced: 135 us -> 25.5 us
  blocking collectives: 72.8 us -> 0 us
  matrix products: 39.6 us -> 0 us
  Pallas kernels: 0 us -> 21.8 us
  local copies, waits for them, and re-layouts: 19.6 us -> 3 us
  other arithmetic: 1.87 us -> 0 us
    all_gather x6 -> x0, blocking collectives: 72.8 us -> none  [merged_2(): pieces = jax.tree.map(lambda part: lax.all_gather(part, axis), value)]
    dot_general x24 -> x0, matrix products: 39.6 us -> none  [the longest x8 16.1 us: centred_add_block(): jnp.dot(hot, centre, precision=HIGHEST, preferred_element_type=jnp.float32)]
    pallas_call x0 -> x1, Pallas kernels: none -> 21.8 us  [on_device(): pl.pallas_call(functools.partial(kernel, axes, sizes, owners, rows), out_...]
    dynamic_slice x16 -> x0, local copies, waits for them, and re-layouts: 11.6 us -> none  [local_moments(): return lax.scan(per_micro, 0.0, (losses, domains))[1]]
    dynamic_update_slice x24 -> x0, local copies, waits for them, and re-layouts: 4.69 us -> none  [local_moments(): return lax.scan(per_micro, 0.0, (losses, domains))[1]]
    slice x15 -> x0, local copies, waits for them, and re-layouts: 1.78 us -> none  [the longest x9 1.65 us: merged_2(): head = jax.tree.map(lambda part: part[0], pieces)]
    unnamed x10 -> x7, local copies, waits for them, and re-layouts: 1.54 us -> 3 us
where the time goes in v1:
time: 25.8 us; the launch traced here: 25.5 us
  Pallas kernels  21.8 us (84%)
  local copies, waits for them, and re-layouts  3 us (12%)
  between operations  0.65 us (3%)
    pallas_call x1, Pallas kernels, on_device(): pl.pallas_call(functools.partial(kernel, axes, sizes, owners, rows), out_...  21.8 us
    unnamed x7, local copies, waits for them, and re-layouts  3 us

profile of v1, /device:TPU:0, one launch (start us, length us, event | category | flops | bytes accessed | tf_op | source)
XLA Modules:
  0.0 25.5 jit_solution(1577970801246003332)
XLA Ops:
  0.6 21.8 %shard_map.49 = (f32[8,2048]{1,0:T(8,128)}, f32[8,2048]{1,0:T(8,128)}, f32[8,2048]{1,0:T(8,128)}) custom-call(f32[8,512]{1,0:T(8,128)} %loss_ref.1, s32[8,512]{1,0:T(8,128)} %ids_ref.1), custom_call_target="tpu_custom_call" | custom-call | tf_op jit(solution)/shard_map/pallas_call | solution.py:174
  22.4 0.0 copy-start.1
  22.4 1.5 %copy.8 = f32[8,2048]{1,0:T(8,128)} copy(f32[8,2048]{1,0:T(8,128)} %get-tuple-element.6) | data formatting | bytes 131072
  24.0 0.0 copy-done.1
  24.0 0.0 copy-start
  24.0 0.6 %copy.9 = f32[8,2048]{1,0:T(8,128)} copy(f32[8,2048]{1,0:T(8,128)S(1)} %copy-done.1) | data formatting | bytes 131072
  24.6 0.2 copy-done
  24.8 0.6 %copy.10 = f32[8,2048]{1,0:T(8,128)} copy(f32[8,2048]{1,0:T(8,128)S(1)} %copy-done) | data formatting | bytes 131072
Async XLA Ops:
  22.4 1.5 %copy-start.1 = (f32[8,2048]{1,0:T(8,128)S(1)}, f32[8,2048]{1,0:T(8,128)}, u32[]{:S(2)}) copy-start(f32[8,2048]{1,0:T(8,128)} %get-tuple-element.7) | copy-start | bytes 196612
  24.0 0.9 %copy-start = (f32[8,2048]{1,0:T(8,128)S(1)}, f32[8,2048]{1,0:T(8,128)}, u32[]{:S(2)}) copy-start(f32[8,2048]{1,0:T(8,128)} %get-tuple-element.8) | copy-start | bytes 196612
